TPU v7x, 256 devices: a whole 4x4x8 slice. The times are simulated.
256 devices in a mesh: owner: 8 (over x, core), rows: 32 (over z, y).
Axes of the slice: x: 4, y: 4, z: 8, core: 2. Of those that a mesh axis runs over, the one named last changes fastest.
Arguments:
- master_gate: float32 [64, 2048, 1408], P('owner', 'rows'), may hold values from -0.25 to 0.25
- master_up: float32 [64, 2048, 1408], P('owner', 'rows'), may hold values from -0.25 to 0.25
- router_weight: float32 [2048, 64], P('rows', 'owner'), may hold values from -0.125 to 0.125
- router_gain: float32 [2048], P('rows'), may hold values from 0.25 to 1.75
Outputs:
- final_gate: bfloat16 [64, 2048, 1408], P('owner', None, 'rows')
- final_up: bfloat16 [64, 2048, 1408], P('owner', None, 'rows')
- scale_gate: float32 [64, 1408], P('owner', 'rows')
- scale_up: float32 [64, 1408], P('owner', 'rows')
- serve_router: bfloat16 [2048, 64], replicated
All inputs are finite; a program needn't handle non-finite values. Where the computation divides by a largest or mean magnitude, that divisor is 1e-20 or more.
Results may differ from a plain program's by a relative error of at most 0.001.
Values may be sent and summed in bfloat16 or wider, within the bound.
A program may use at most 64 MiB of HBM per device.

v0:
```python
import jax
import jax.numpy as jnp
from jax import lax
from jax.sharding import Mesh
from jax.sharding import PartitionSpec as P

OWNER = ("owner_0", "owner_1")


def sent_to_all(value, axis):
    copies = jnp.broadcast_to(value, (lax.axis_size(axis), *value.shape))
    return lax.all_to_all(copies, axis, split_axis=0, concat_axis=0, tiled=True)


def over_copies(value, axis):
    return sent_to_all(value, axis).max(axis=0)


def packed_total(arrays, axis):
    ends = [0]
    for a in arrays:
        ends.append(ends[-1] + a.size)
    running = over_copies(jnp.concatenate([a.ravel() for a in arrays]), axis)
    return tuple((running[b:e].reshape(a.shape) for a, b, e in zip(arrays, ends, ends[1:])))


def joined_along(pieces, dim):
    lengths = list(pieces.shape[1:])
    lengths[dim] *= pieces.shape[0]
    return jnp.moveaxis(pieces, 0, dim).reshape(lengths)


def collect(value, axis, dim):
    pieces = sent_to_all(value, axis)
    return joined_along(pieces, dim)


def all_blocks(value, axes, turns):
    pieces = value
    for k in turns:
        pieces = lax.all_gather(pieces, axes[k])
    done = turns[::-1]
    back = [done.index(k) for k in range(len(axes))]
    pieces = pieces.transpose(*back, *range(len(axes), pieces.ndim))
    return pieces.reshape(-1, *value.shape)


def whole_of(value, axes, turns, dim):
    return joined_along(all_blocks(value, axes, turns), dim)


def shards(master_gate, master_up, router_weight, router_gain):
    scale_gate, scale_up = packed_total(
        (jnp.max(jnp.abs(master_gate), axis=1), jnp.max(jnp.abs(master_up), axis=1)), "rows"
    )
    narrow_gate, narrow_up = (
        (master_gate / jnp.expand_dims(scale_gate, 1)).astype(jnp.bfloat16),
        (master_up / jnp.expand_dims(scale_up, 1)).astype(jnp.bfloat16),
    )
    final_gate, final_up = (
        lax.all_to_all(narrow_gate, "rows", split_axis=2, concat_axis=1, tiled=True),
        lax.all_to_all(narrow_up, "rows", split_axis=2, concat_axis=1, tiled=True),
    )
    scale_gate = lax.dynamic_slice_in_dim(
        scale_gate, lax.axis_index("rows") * final_gate.shape[2], final_gate.shape[2], axis=1
    )
    scale_up = lax.dynamic_slice_in_dim(
        scale_up, lax.axis_index("rows") * final_up.shape[2], final_up.shape[2], axis=1
    )
    part_router = (router_weight * router_gain[:, None]).astype(jnp.bfloat16)
    row_router = collect(part_router, "rows", 0)
    serve_router = whole_of(row_router, ("owner_0", "owner_1"), (0, 1), 1)
    return (final_gate, final_up, scale_gate, scale_up, serve_router)


def solution(mesh):
    finer = Mesh(mesh.devices.reshape(4, 2, mesh.shape["rows"]), ("owner_0", "owner_1", "rows"))
    return jax.shard_map(
        shards,
        mesh=finer,
        in_specs=(P(OWNER, "rows", None), P(OWNER, "rows", None), P("rows", OWNER), P("rows")),
        out_specs=(
            P(OWNER, None, "rows"),
            P(OWNER, None, "rows"),
            P(OWNER, "rows"),
            P(OWNER, "rows"),
            P(),
        ),
        check_vma=False,
    )
```

profile of v0, /device:TPU:14, one launch (start us, length us, event | category | flops | bytes accessed | tf_op | source)
XLA Modules:
  0.0 203.3 jit_solution(14196817767475329260)
XLA Ops:
  0.6 0.0 copy-start.1
  0.6 2.2 %abs_reduce_fusion.1 = f32[8,1408]{1,0:T(8,128)S(1)} fusion(f32[8,64,1408]{2,1,0:T(8,128)} %param.4), kind=kLoop, calls=%fused_computation.3 | loop fusion | flops 1430528 | bytes 2928640 | tf_op jit(solution)/shard_map/reduce_max | solution.py:54
  2.9 0.5 copy-done.1
  3.3 0.2 abs_reduce_fusion
  3.6 3.1 %broadcast_in_dim.7 = f32[32,1,22528]{2,1,0:T(1,128)} broadcast(f32[22528]{0:T(1024)S(1)} %pad_maximum_fusion), dimensions={2} | broadcast | bytes 2973696 | tf_op jit(solution)/shard_map/broadcast_in_dim | solution.py:11
  6.7 0.0 copy-start
  6.7 12.0 %all-to-all-start = ((f32[32,1,22528]{2,1,0:T(1,128)}), f32[32,1,22528]{2,1,0:T(1,128)}, u32[]{:S(2)}, u32[]{:S(2)}) async-start(f32[32,1,22528]{2,1,0:T(1,128)} %broadcast_in_dim.7), calls=%async_computation | async-start | bytes 5767168 | tf_op jit(solution)/shard_map/all_to_all | solution.py:12
  18.7 0.0 copy-done
  18.8 0.0 copy-start.3
  18.8 0.0 copy-start.4
  18.8 4.1 %copy.48 = f32[8,64,1408]{1,0,2:T(8,128)} copy(f32[8,64,1408]{2,1,0:T(8,128)S(1)} %copy-done) | data formatting | bytes 5767168 | tf_op args[0]
  22.9 0.0 copy-done.3
  22.9 0.0 copy-done.4
  22.9 0.7 reshape.60
  23.7 60.8 %all-to-all-done = f32[32,1,22528]{2,1,0:T(1,128)} async-done(((f32[32,1,22528]{2,1,0:T(1,128)}), f32[32,1,22528]{2,1,0:T(1,128)}, u32[]{:S(2)}, u32[]{:S(2)}) %all-to-all-start) | async-done | bytes 2883616 | tf_op jit(solution)/shard_map/all_to_all | solution.py:12
  84.5 7.3 %all-to-all-start.3 = ((bf16[32,2,256]{2,1,0:T(2,128)(2,1)}), bf16[32,2,256]{2,1,0:T(2,128)(2,1)S(1)}, u32[]{:S(2)}, u32[]{:S(2)}) async-start(bf16[32,2,256]{2,1,0:T(2,128)(2,1)} %reshape.60), calls=%async_computation.3 | async-start | bytes 65536 | tf_op jit(solution)/shard_map/all_to_all | solution.py:12
  91.8 3.5 %reduce_max.29 = f32[22528]{0:T(1024)S(1)} reduce(f32[32,1,22528]{2,1,0:T(1,128)} %all-to-all-done, f32[]{:T(128)} %constant.5.clone.1), dimensions={0,1}, to_apply=%region_2.0 | reduce | flops 698368 | bytes 2973700 | tf_op jit(solution)/shard_map/reduce_max | solution.py:16
  95.3 0.3 copy.47
  95.5 6.6 %fusion.1 = bf16[1408,8,64]{2,1,0:T(8,128)(2,1)} fusion(f32[8,64,1408]{1,0,2:T(8,128)} %copy.48, f32[8,1408]{0,1:T(8,128)S(1)} %copy.47), kind=kLoop, calls=%fused_computation.9 | loop fusion | flops 1441792 | bytes 4370432
  102.1 0.0 copy-start.2
  102.1 4.8 %reshape.56 = bf16[32,2,11264]{2,1,0:T(2,128)(2,1)} reshape(bf16[1408,8,64]{2,1,0:T(8,128)(2,1)} %fusion.1) | data formatting | bytes 2883584
  106.9 0.0 all-to-all-done.3
  106.9 9.8 %all-to-all-start.1 = ((bf16[32,2,11264]{2,1,0:T(2,128)(2,1)}), bf16[32,2,11264]{2,1,0:T(2,128)(2,1)}, u32[]{:S(2)}, u32[]{:S(2)}) async-start(bf16[32,2,11264]{2,1,0:T(2,128)(2,1)} %reshape.56), calls=%async_computation.1 | async-start | bytes 2883584 | tf_op jit(solution)/shard_map/all_to_all | solution.py:61
  116.7 0.0 copy-done.2
  116.7 4.1 %copy.51 = f32[8,64,1408]{1,0,2:T(8,128)} copy(f32[8,64,1408]{2,1,0:T(8,128)S(1)} %copy-done.2) | data formatting | bytes 5767168 | tf_op args[1]
  120.9 1.1 copy.50
  122.0 4.7 %fusion.2 = bf16[1408,8,64]{2,1,0:T(8,128)(2,1)S(1)} fusion(f32[8,64,1408]{1,0,2:T(8,128)} %copy.51, f32[8,1408]{0,1:T(8,128)} %copy.50), kind=kLoop, calls=%fused_computation.10 | loop fusion | flops 1441792 | bytes 4370432
  126.7 2.8 %reshape.58 = bf16[32,2,11264]{2,1,0:T(2,128)(2,1)} reshape(bf16[1408,8,64]{2,1,0:T(8,128)(2,1)S(1)} %fusion.2) | data formatting | bytes 2883584
  129.6 22.1 %all-to-all-done.1 = bf16[32,2,11264]{2,1,0:T(2,128)(2,1)} async-done(((bf16[32,2,11264]{2,1,0:T(2,128)(2,1)}), bf16[32,2,11264]{2,1,0:T(2,128)(2,1)}, u32[]{:S(2)}, u32[]{:S(2)}) %all-to-all-start.1) | async-done | bytes 1441824 | tf_op jit(solution)/shard_map/all_to_all | solution.py:61
  151.6 6.1 %all-to-all-start.2 = ((bf16[32,2,11264]{2,1,0:T(2,128)(2,1)}), bf16[32,2,11264]{2,1,0:T(2,128)(2,1)}, u32[]{:S(2)}, u32[]{:S(2)}) async-start(bf16[32,2,11264]{2,1,0:T(2,128)(2,1)} %reshape.58), calls=%async_computation.2 | async-start | bytes 2883584 | tf_op jit(solution)/shard_map/all_to_all | solution.py:62
  157.7 0.1 reshape.61
  157.9 0.1 all_gather_reshape.3
  158.0 12.0 %all_gather.9 = bf16[4,2048,8]{1,2,0:T(8,128)(2,1)S(1)} all-gather(bf16[1,2048,8]{1,2,0:T(8,128)(2,1)S(1)} %all_gather_reshape.3), channel_id=1, replica_groups=mesh['owner_0'=4,'owner_1'=2,'rows'=32] {'owner_0'}, dimensions={0}, use_global_device_ids=true | all-gather | bytes 163840 | tf_op jit(solution)/shard_map/all_gather | solution.py:41
  170.0 2.2 %all-gather = bf16[8,2048,8]{1,2,0:T(8,128)(2,1)S(1)} all-gather(bf16[4,2048,8]{1,2,0:T(8,128)(2,1)S(1)} %all_gather.9), channel_id=2, replica_groups=mesh['owner_0'=4,'owner_1'=2,'rows'=32] {'owner_1'}, dimensions={0}, use_global_device_ids=true | all-gather | bytes 393216 | tf_op jit(solution)/shard_map/all_gather | solution.py:41
  172.2 0.7 copy.54
  172.9 0.7 constant_dynamic-slice_fusion
  173.5 3.5 %reshape.57 = bf16[1408,8,64]{2,1,0:T(8,128)(2,1)S(1)} reshape(bf16[32,2,11264]{2,1,0:T(2,128)(2,1)} %all-to-all-done.1) | data formatting | bytes 2883584
  177.0 2.7 %copy.49 = bf16[8,32,64,44]{2,1,0,3:T(8,128)(2,1)} copy(bf16[8,32,64,44]{2,0,3,1:T(8,128)(2,1)S(1)} %bitcast.33) | data formatting | bytes 2883584 | tf_op jit(solution)/shard_map/all_to_all | solution.py:61
  179.7 4.9 %all_to_all.37 = bf16[8,2048,44]{1,0,2:T(8,128)(2,1)} reshape(bf16[8,32,64,44]{2,1,0,3:T(8,128)(2,1)} %copy.49) | data formatting | bytes 2883584 | tf_op jit(solution)/shard_map/all_to_all | solution.py:61
  184.7 7.5 %all-to-all-done.2 = bf16[32,2,11264]{2,1,0:T(2,128)(2,1)} async-done(((bf16[32,2,11264]{2,1,0:T(2,128)(2,1)}), bf16[32,2,11264]{2,1,0:T(2,128)(2,1)}, u32[]{:S(2)}, u32[]{:S(2)}) %all-to-all-start.2) | async-done | bytes 1441824 | tf_op jit(solution)/shard_map/all_to_all | solution.py:62
  192.1 3.5 %reshape.59 = bf16[1408,8,64]{2,1,0:T(8,128)(2,1)S(1)} reshape(bf16[32,2,11264]{2,1,0:T(2,128)(2,1)} %all-to-all-done.2) | data formatting | bytes 2883584
  195.6 2.7 %copy.52 = bf16[8,32,64,44]{2,1,0,3:T(8,128)(2,1)} copy(bf16[8,32,64,44]{2,0,3,1:T(8,128)(2,1)S(1)} %bitcast.34) | data formatting | bytes 2883584 | tf_op jit(solution)/shard_map/all_to_all | solution.py:62
  198.3 4.9 %all_to_all.41 = bf16[8,2048,44]{1,0,2:T(8,128)(2,1)} reshape(bf16[8,32,64,44]{2,1,0,3:T(8,128)(2,1)} %copy.52) | data formatting | bytes 2883584 | tf_op jit(solution)/shard_map/all_to_all | solution.py:62
  (9 shorter events, 0.1 us)
Async XLA Ops:
  0.6 2.7 %copy-start.1 = (f32[8,64,1408]{2,1,0:T(8,128)S(1)}, f32[8,64,1408]{2,1,0:T(8,128)}, u32[]{:S(2)}) copy-start(f32[8,64,1408]{2,1,0:T(8,128)} %param.5) | copy-start | bytes 8650756
  6.7 12.0 %copy-start = (f32[8,64,1408]{2,1,0:T(8,128)S(1)}, f32[8,64,1408]{2,1,0:T(8,128)}, u32[]{:S(2)}) copy-start(f32[8,64,1408]{2,1,0:T(8,128)} %param.4) | copy-start | bytes 8650756
  6.7 77.8 %all-to-all-start = ((f32[32,1,22528]{2,1,0:T(1,128)}), f32[32,1,22528]{2,1,0:T(1,128)}, u32[]{:S(2)}, u32[]{:S(2)}) async-start(f32[32,1,22528]{2,1,0:T(1,128)} %broadcast_in_dim.7), calls=%async_computation | async-start | bytes 5767168 | tf_op jit(solution)/shard_map/all_to_all | solution.py:12
  18.8 4.1 %copy-start.3 = (f32[64,8]{0,1:T(8,128)S(1)}, f32[64,8]{0,1:T(8,128)}, u32[]{:S(2)}) copy-start(f32[64,8]{0,1:T(8,128)} %param.6) | copy-start | bytes 6148
  18.8 4.1 %copy-start.4 = (f32[64]{0:T(128)S(1)}, f32[64]{0:T(128)}, u32[]{:S(2)}) copy-start(f32[64]{0:T(128)} %param.7) | copy-start | bytes 772
  84.5 22.4 %all-to-all-start.3 = ((bf16[32,2,256]{2,1,0:T(2,128)(2,1)}), bf16[32,2,256]{2,1,0:T(2,128)(2,1)S(1)}, u32[]{:S(2)}, u32[]{:S(2)}) async-start(bf16[32,2,256]{2,1,0:T(2,128)(2,1)} %reshape.60), calls=%async_computation.3 | async-start | bytes 65536 | tf_op jit(solution)/shard_map/all_to_all | solution.py:12
  102.1 14.6 %copy-start.2 = (f32[8,64,1408]{2,1,0:T(8,128)S(1)}, f32[8,64,1408]{2,1,0:T(8,128)}, u32[]{:S(2)}) copy-start(f32[8,64,1408]{2,1,0:T(8,128)} %param.5) | copy-start | bytes 8650756
  106.9 44.8 %all-to-all-start.1 = ((bf16[32,2,11264]{2,1,0:T(2,128)(2,1)}), bf16[32,2,11264]{2,1,0:T(2,128)(2,1)}, u32[]{:S(2)}, u32[]{:S(2)}) async-start(bf16[32,2,11264]{2,1,0:T(2,128)(2,1)} %reshape.56), calls=%async_computation.1 | async-start | bytes 2883584 | tf_op jit(solution)/shard_map/all_to_all | solution.py:61
  151.6 40.5 %all-to-all-start.2 = ((bf16[32,2,11264]{2,1,0:T(2,128)(2,1)}), bf16[32,2,11264]{2,1,0:T(2,128)(2,1)}, u32[]{:S(2)}, u32[]{:S(2)}) async-start(bf16[32,2,11264]{2,1,0:T(2,128)(2,1)} %reshape.58), calls=%async_computation.2 | async-start | bytes 2883584 | tf_op jit(solution)/shard_map/all_to_all | solution.py:62
where the time goes:
time: 204 us; the launch traced here: 203 us
  waiting for transfers between devices  90.4 us (44%)
  local copies, waits for them, and re-layouts  45.5 us (22%)
  starting transfers between devices  35.2 us (17%)
  other arithmetic  17.2 us (8%)
  blocking collectives  14.2 us (7%)
    all_to_all x2, waiting for transfers between devices, sent_to_all(): return lax.all_to_all(copies, axis, split_axis=0, concat_axis=0, tiled=True)  60.8 us
    unnamed x19, local copies, waits for them, and re-layouts  24.2 us
    all_to_all x1, waiting for transfers between devices, shards(): lax.all_to_all(narrow_gate, 'rows', split_axis=2, concat_axis=1, tiled=True)  22.1 us
    all_to_all x2, starting transfers between devices, sent_to_all(): return lax.all_to_all(copies, axis, split_axis=0, concat_axis=0, tiled=True)  19.3 us
    all_gather x2, blocking collectives, all_blocks(): pieces = lax.all_gather(pieces, axes[k])  14.2 us
    unnamed x2, other arithmetic  11.3 us
    all_to_all x1, starting transfers between devices, shards(): lax.all_to_all(narrow_gate, 'rows', split_axis=2, concat_axis=1, tiled=True)  9.82 us
    all_to_all x2, local copies, waits for them, and re-layouts, shards(): lax.all_to_all(narrow_gate, 'rows', split_axis=2, concat_axis=1, tiled=True)  7.62 us
  transfers between devices with their start and end apart: 4, of which 3 were waited for; matrix products, arithmetic and copies ran while one was open for 20% of the time, Pallas kernels for 0%

commit v1 on v0

v1 whole, which is shorter than its diff:
```python
import jax
import jax.numpy as jnp
from jax import lax
from jax.experimental import pallas as pl
from jax.experimental.pallas import tpu as pltpu
from jax.sharding import PartitionSpec as P

MESH = pl.DeviceIdType.MESH
ROWS, OWNERS = 32, 8
E, R, D = 8, 64, 1408
C = D // ROWS
TILES = D // 128
Q = 2 * TILES
MSG = C * E


def owner_of(q):
    return (q * 16) // 11


def remote(src, dst, send, recv, **where):
    return pltpu.make_async_remote_copy(
        src_ref=src, dst_ref=dst, send_sem=send, recv_sem=recv, device_id=where, device_id_type=MESH
    )


def exchange(gate, up, rw, gain, fg, fu, sc_out, sr,
             x, w, xn, ml, parts, sc, rr, s, r, own, rpiece, rparts, rrow, rall,
             in_sem, a_send, a_recv, b_send, b_recv, s_send, s_recv, p_send, p_recv, o_send, o_recv):
    me = lax.axis_index("rows")
    us = lax.axis_index("owner")
    par = lax.rem(me, 2)

    def peer(k):
        return lax.rem(me + k, ROWS)

    loads = []
    for e in range(E):
        for a, ref in enumerate((gate, up)):
            cp = pltpu.make_async_copy(ref.at[e], x.at[a, e], in_sem.at[a, e])
            cp.start()
            loads.append((a, e, cp))
    barrier = pltpu.get_barrier_semaphore()

    def signal_rows(k, _):
        pl.semaphore_signal(barrier, inc=1, device_id={"rows": peer(k)}, device_id_type=MESH)
        return 0

    lax.fori_loop(1, ROWS, signal_rows, 0)

    def signal_owner(k, _):
        pl.semaphore_signal(barrier, inc=1, device_id={"owner": lax.rem(us + k, OWNERS)}, device_id_type=MESH)
        return 0

    lax.fori_loop(1, OWNERS, signal_owner, 0)

    part = rw[...] * gain[...]
    lane64 = lax.broadcasted_iota(jnp.int32, (E, 128), 1) // 64
    rpiece[...] = jnp.where(lane64 == par, jnp.concatenate([part, part], axis=1), 0.0)
    for m in range(8):
        i = lax.broadcasted_iota(jnp.int32, (128, 1024), 0) + m * 128
        k = lax.broadcasted_iota(jnp.int32, (128, 1024), 1)
        hit = (lax.rem(i, 8) == k // 128) & (i // 8 == lax.rem(k, 128))
        w[pl.ds(m * 128, 128), :] = jnp.where(hit, 1.0, 0.0).astype(jnp.bfloat16)
    for a, e, cp in loads:
        cp.wait()
        m = jnp.max(jnp.abs(x[a, e]), axis=0, keepdims=True)
        for t in range(TILES):
            ml[a * TILES + t, pl.ds(e, 1), :] = m[:, t * 128:(t + 1) * 128]

    pl.semaphore_wait(barrier, ROWS - 1 + OWNERS - 1)

    def send_part(q, _):
        to = owner_of(q)

        @pl.when(to != me)
        def _():
            remote(ml.at[q], parts.at[me], a_send.at[q], a_recv.at[me], rows=to).start()

        @pl.when(to == me)
        def _():
            parts[pl.ds(me, 1)] = ml[pl.ds(q, 1)]

        return 0

    lax.fori_loop(0, Q, send_part, 0)

    def send_router(k, _):
        to = peer(k)
        remote(rpiece, rparts.at[me], p_send.at[k], p_recv.at[me], rows=to).start()
        return 0

    lax.fori_loop(1, ROWS, send_router, 0)
    rparts[pl.ds(me, 1)] = rpiece[...][None]

    mine = (11 * me + 15) // 16
    is_owner = owner_of(mine) == me

    @pl.when(is_owner)
    def _():
        def wait_part(k, _):
            src = peer(k)
            remote(ml.at[0], parts.at[src], a_send.at[0], a_recv.at[src], rows=src).wait_recv()
            return 0

        lax.fori_loop(1, ROWS, wait_part, 0)
        sc[pl.ds(mine, 1)] = jnp.max(parts[...], axis=0, keepdims=True)

        def send_scale(k, _):
            remote(sc.at[mine], sc.at[mine], b_send.at[k], b_recv.at[mine], rows=peer(k)).start()
            return 0

        lax.fori_loop(1, ROWS, send_scale, 0)

    def wait_scale(q, _):
        @pl.when(owner_of(q) != me)
        def _():
            remote(sc.at[q], sc.at[q], b_send.at[0], b_recv.at[q], rows=owner_of(q)).wait_recv()

        return 0

    lax.fori_loop(0, Q, wait_scale, 0)
    rr[...] = 1.0 / sc[...]

    for t0 in range(0, TILES, 2):
        n = min(2, TILES - t0)
        for i in range(n):
            t = t0 + i
            for h in range(2):
                a = lax.rem(par + h, 2)
                for e in range(E):
                    v = x[a, e, :, t * 128:(t + 1) * 128] * rr[a * TILES + t, pl.ds(e, 1), :]
                    xn[pl.ds(i * 128 + h * 64, 64), e * 128:(e + 1) * 128] = v.astype(jnp.bfloat16)
        out = lax.dot_general(
            w[...], xn[:n * 128, :], (((1,), (1,)), ((), ())), preferred_element_type=jnp.float32
        )
        for i in range(n):
            s[pl.ds((t0 + i) * 1024, 1024), :] = out[:, i * 128:(i + 1) * 128].astype(jnp.bfloat16)

    def block(j):
        return s.at[pl.ds(pl.multiple_of(j * MSG, 32), MSG)]

    def send_block(k, _):
        to = peer(k)
        remote(block(to), r.at[me], s_send.at[k], s_recv.at[me], rows=to).start()
        return 0

    lax.fori_loop(1, ROWS, send_block, 0)
    keep = pltpu.make_async_copy(block(me), r.at[me], s_recv.at[me])
    keep.start()

    first = (C * me) // 128
    second = jnp.minimum(first + 1, TILES - 1)
    shift = lax.rem(256 - (C * me - 128 * first), 256)
    for a in range(2):
        both = jnp.concatenate([sc[a * TILES + first], sc[a * TILES + second]], axis=1)
        sc_out[a] = pltpu.roll(both, shift, 1)[:, :128]

    def wait_router(k, _):
        src = peer(k)
        remote(rpiece, rparts.at[src], p_send.at[0], p_recv.at[src], rows=src).wait_recv()
        return 0

    lax.fori_loop(1, ROWS, wait_router, 0)
    for p in range(ROWS // 2):
        rrow[:, p * 128:(p + 1) * 128] = rparts[2 * p] + rparts[2 * p + 1]
    for k in range(1, OWNERS):
        to = lax.rem(us + k, OWNERS)
        remote(rrow, rall.at[us], o_send.at[k], o_recv.at[us], owner=to).start()
    rall[pl.ds(us, 1)] = rrow[...][None]

    lane = lax.broadcasted_iota(jnp.int32, (MSG, 128), 1) < 64

    def merge(kk, _):
        p = lax.rem(me // 2 - kk + 16, 16)
        for src in (2 * p, 2 * p + 1):
            pltpu.make_async_copy(r.at[src], r.at[src], s_recv.at[src]).wait()
        even, odd = r[2 * p].astype(jnp.float32), r[2 * p + 1].astype(jnp.float32)
        at = pl.ds(pl.multiple_of(p * 128, 128), 128)
        fg[:, at] = jnp.where(lane, even, odd).astype(jnp.bfloat16)
        fu[:, at] = pltpu.roll(jnp.where(lane, odd, even), 64, 1).astype(jnp.bfloat16)
        return 0

    lax.fori_loop(1, ROWS // 2 + 1, merge, 0)

    for k in range(1, OWNERS):
        src = lax.rem(us + k, OWNERS)
        remote(rrow, rall.at[src], o_send.at[k], o_recv.at[src], owner=src).wait_recv()
    for o in range(OWNERS):
        sr[o * E:(o + 1) * E, :] = rall[o].astype(jnp.bfloat16)

    def drain_a(q, _):
        @pl.when(owner_of(q) != me)
        def _():
            remote(ml.at[q], parts.at[me], a_send.at[q], a_recv.at[me], rows=owner_of(q)).wait_send()

        return 0

    lax.fori_loop(0, Q, drain_a, 0)

    @pl.when(is_owner)
    def _():
        def drain_b(k, _):
            remote(sc.at[mine], sc.at[mine], b_send.at[k], b_recv.at[mine], rows=peer(k)).wait_send()
            return 0

        lax.fori_loop(1, ROWS, drain_b, 0)

    def drain(k, _):
        to = peer(k)
        remote(rpiece, rparts.at[me], p_send.at[k], p_recv.at[me], rows=to).wait_send()
        remote(block(to), r.at[me], s_send.at[k], s_recv.at[me], rows=to).wait_send()
        return 0

    lax.fori_loop(1, ROWS, drain, 0)
    for k in range(1, OWNERS):
        to = lax.rem(us + k, OWNERS)
        remote(rrow, rall.at[us], o_send.at[k], o_recv.at[us], owner=to).wait_send()


def put_out(*refs):
    ins, outs, sem = refs[:5], refs[5:10], refs[10]
    copies = [pltpu.make_async_copy(i, o, sem.at[n]) for n, (i, o) in enumerate(zip(ins, outs))]
    for cp in copies:
        cp.start()
    for cp in copies:
        cp.wait()


def shards(master_gate, master_up, router_weight, router_gain):
    f32, bf16 = jnp.float32, jnp.bfloat16
    vmem, any_ = pl.BlockSpec(memory_space=pltpu.VMEM), pl.BlockSpec(memory_space=pl.ANY)
    dma, scratch = pltpu.SemaphoreType.DMA, pltpu.VMEM
    fg, fu, sc, sr = pl.pallas_call(
        exchange,
        name="exchange",
        out_shape=(
            jax.ShapeDtypeStruct((MSG, ROWS * R), bf16),
            jax.ShapeDtypeStruct((MSG, ROWS * R), bf16),
            jax.ShapeDtypeStruct((2, E, 128), f32),
            jax.ShapeDtypeStruct((OWNERS * E, ROWS * R), bf16),
        ),
        in_specs=[any_, any_, vmem, vmem],
        out_specs=(vmem,) * 4,
        scratch_shapes=[
            scratch((2, E, R, D), f32),
            scratch((1024, 1024), bf16),
            scratch((256, 1024), bf16),
            scratch((Q, E, 128), f32),
            scratch((ROWS, E, 128), f32),
            scratch((Q, E, 128), f32),
            scratch((Q, E, 128), f32),
            scratch((D * E, 128), bf16),
            scratch((ROWS, MSG, 128), bf16),
            scratch((2, E, 128), f32),
            scratch((E, 128), f32),
            scratch((ROWS, E, 128), f32),
            scratch((E, ROWS * R), f32),
            scratch((OWNERS, E, ROWS * R), f32),
            dma((2, E)), dma((Q,)), dma((ROWS,)), dma((ROWS,)), dma((Q,)),
            dma((ROWS,)), dma((ROWS,)), dma((ROWS,)), dma((ROWS,)), dma((OWNERS,)), dma((OWNERS,)),
        ],
        compiler_params=pltpu.CompilerParams(
            collective_id=0, has_side_effects=True, vmem_limit_bytes=40 * 2**20
        ),
    )(master_gate, master_up, router_weight.T, router_gain[None, :])
    sg, su = sc[0, :, :C], sc[1, :, :C]
    fg, fu = fg.reshape(C, E, ROWS * R), fu.reshape(C, E, ROWS * R)
    ins = (fg, fu, sg, su, sr)
    fg, fu, sg, su, sr = pl.pallas_call(
        put_out,
        name="put_out",
        out_shape=tuple(jax.ShapeDtypeStruct(i.shape, i.dtype) for i in ins),
        in_specs=[vmem] * 5,
        out_specs=(any_,) * 5,
        scratch_shapes=[dma((5,))],
    )(*ins)
    return fg.transpose(1, 2, 0), fu.transpose(1, 2, 0), sg, su, sr.T


def solution(mesh):
    return jax.shard_map(
        shards,
        mesh=mesh,
        in_specs=(P("owner", "rows", None), P("owner", "rows", None), P("rows", "owner"), P("rows")),
        out_specs=(
            P("owner", None, "rows"), P("owner", None, "rows"), P("owner", "rows"), P("owner", "rows"), P(),
        ),
        check_vma=False,
    )
```

time: 204 us -> 109 us (0.53)
  Pallas kernels: 0 us -> 99.3 us
  waiting for transfers between devices: 90.4 us -> 0 us
  local copies, waits for them, and re-layouts: 45.5 us -> 8.49 us
  starting transfers between devices: 35.2 us -> 0 us
  other arithmetic: 17.2 us -> 0 us
  blocking collectives: 14.2 us -> 0 us
    pallas_call x0 -> x2, Pallas kernels: none -> 99.3 us  [the longest x1 95.8 us: shards(): pl.pallas_call(exchange, name='exchange', out_shape=(jax.ShapeDtypeStruct...]
    all_to_all x4 -> x0, waiting for transfers between devices: 90.4 us -> none  [the longest x2 60.8 us: sent_to_all(): return lax.all_to_all(copies, axis, split_axis=0, concat_axis=0, tiled=True)]
    all_to_all x4 -> x0, starting transfers between devices: 35.2 us -> none  [the longest x2 19.3 us: sent_to_all(): return lax.all_to_all(copies, axis, split_axis=0, concat_axis=0, tiled=True)]
    unnamed x19 -> x14, local copies, waits for them, and re-layouts: 24.2 us -> 7.89 us
    all_to_all x5 -> x0, local copies, waits for them, and re-layouts: 15.3 us -> none  [the longest x2 7.62 us: shards(): lax.all_to_all(narrow_gate, 'rows', split_axis=2, concat_axis=1, tiled=True)]
    all_gather x2 -> x0, blocking collectives: 14.2 us -> none  [all_blocks(): pieces = lax.all_gather(pieces, axes[k])]
    unnamed x2 -> x0, other arithmetic: 11.3 us -> none
    reduce_max x3 -> x0, other arithmetic: 5.87 us -> none  [the longest x1 3.45 us: over_copies(): return sent_to_all(value, axis).max(axis=0)]
  transfers between devices with their start and end apart: 4 -> 0, of which waited for: 3 -> 0; matrix products, arithmetic and copies ran while one was open for 20% -> 0% of each run, Pallas kernels for 0% -> 0%
where the time goes in v1:
time: 109 us; the launch traced here: 108 us
  Pallas kernels  99.3 us (91%)
  local copies, waits for them, and re-layouts  8.49 us (8%)
    pallas_call x1, Pallas kernels, shards(): pl.pallas_call(exchange, name='exchange', out_shape=(jax.ShapeDtypeStruct...  95.8 us
    unnamed x14, local copies, waits for them, and re-layouts  7.89 us
    pallas_call x1, Pallas kernels, shards(): pl.pallas_call(put_out, name='put_out', out_shape=tuple((jax.ShapeDtypeSt...  3.53 us

profile of v1, /device:TPU:14, one launch (start us, length us, event | category | flops | bytes accessed | tf_op | source)
XLA Modules:
  0.0 108.4 jit_solution(15639982936129389341)
XLA Ops:
  0.6 0.0 copy-start
  0.6 1.8 %copy-done = f32[8,64,1408]{2,1,0:T(8,128)S(1)} copy-done((f32[8,64,1408]{2,1,0:T(8,128)S(1)}, f32[8,64,1408]{2,1,0:T(8,128)}, u32[]{:S(2)}) %copy-start) | copy-done | bytes 2883608
  2.4 0.0 copy-start.1
  2.5 1.8 %copy-done.1 = f32[8,64,1408]{2,1,0:T(8,128)S(1)} copy-done((f32[8,64,1408]{2,1,0:T(8,128)S(1)}, f32[8,64,1408]{2,1,0:T(8,128)}, u32[]{:S(2)}) %copy-start.1) | copy-done | bytes 2883608
  4.3 0.0 copy-start.5
  4.3 0.7 copy-done.5
  5.0 0.0 copy-start.6
  5.0 0.7 copy-done.6
  5.6 95.8 %exchange.1 = (bf16[352,2048]{1,0:T(8,128)(2,1)S(1)}, bf16[352,2048]{1,0:T(8,128)(2,1)S(1)}, f32[2,8,128]{2,1,0:T(8,128)S(1)}, bf16[64,2048]{1,0:T(8,128)(2,1)S(1)}) custom-call(f32[8,64,1408]{2,1,0:T(8,128)S(1)} %copy-done, f32[8,64,1408]{2,1,0:T(8,128)S(1)} %copy-done.1, f32[8,64]{1,0:T(8,128)S(1)} %bitcast.13, f32[1,64]{1,0:T(1,128)S(1)} %bitcast.14), custom_call_target="tpu_custom_call" | custom-call | tf_op jit(solution)/shard_map/exchange/pallas_call | solution.py:234
  101.4 0.0 copy-start.2
  101.4 1.1 %copy-done.2 = bf16[352,2048]{1,0:T(8,128)(2,1)} copy-done((bf16[352,2048]{1,0:T(8,128)(2,1)}, bf16[352,2048]{1,0:T(8,128)(2,1)S(1)}, u32[]{:S(2)}) %copy-start.2) | copy-done | bytes 1441816
  102.5 0.0 copy-start.3
  102.5 1.1 %copy-done.3 = bf16[352,2048]{1,0:T(8,128)(2,1)} copy-done((bf16[352,2048]{1,0:T(8,128)(2,1)}, bf16[352,2048]{1,0:T(8,128)(2,1)S(1)}, u32[]{:S(2)}) %copy-start.3) | copy-done | bytes 1441816
  103.6 0.0 copy-start.4
  103.6 0.7 copy-done.4
  104.3 0.6 slice_bitcast_fusion
  104.9 3.5 %put_out.1 = (bf16[44,8,2048]{2,1,0:T(8,128)(2,1)}, bf16[44,8,2048]{2,1,0:T(8,128)(2,1)}, f32[8,44]{1,0:T(8,128)}, f32[8,44]{1,0:T(8,128)}, bf16[64,2048]{1,0:T(8,128)(2,1)}) custom-call(bf16[44,8,2048]{2,1,0:T(8,128)(2,1)} %bitcast.11, bf16[44,8,2048]{2,1,0:T(8,128)(2,1)} %bitcast.12, f32[8,44]{1,0:T(8,128)} %get-tuple-element.24.refs_2_, ...), custom_call_target="tpu_custom_call" | custom-call | tf_op jit(solution)/shard_map/put_out/pallas_call | solution.py:270
Async XLA Ops:
  0.6 1.8 %copy-start = (f32[8,64,1408]{2,1,0:T(8,128)S(1)}, f32[8,64,1408]{2,1,0:T(8,128)}, u32[]{:S(2)}) copy-start(f32[8,64,1408]{2,1,0:T(8,128)} %gate.1) | copy-start | bytes 8650756
  2.4 1.8 %copy-start.1 = (f32[8,64,1408]{2,1,0:T(8,128)S(1)}, f32[8,64,1408]{2,1,0:T(8,128)}, u32[]{:S(2)}) copy-start(f32[8,64,1408]{2,1,0:T(8,128)} %up.1) | copy-start | bytes 8650756
  4.3 0.7 copy-start.5
  5.0 0.7 copy-start.6
  101.4 1.1 %copy-start.2 = (bf16[352,2048]{1,0:T(8,128)(2,1)}, bf16[352,2048]{1,0:T(8,128)(2,1)S(1)}, u32[]{:S(2)}) copy-start(bf16[352,2048]{1,0:T(8,128)(2,1)S(1)} %get-tuple-element.14) | copy-start | bytes 4325380
  102.5 1.1 %copy-start.3 = (bf16[352,2048]{1,0:T(8,128)(2,1)}, bf16[352,2048]{1,0:T(8,128)(2,1)S(1)}, u32[]{:S(2)}) copy-start(bf16[352,2048]{1,0:T(8,128)(2,1)S(1)} %get-tuple-element.15) | copy-start | bytes 4325380
  103.6 0.7 copy-start.4

commit v2 on v1

--- a/solution.py
+++ b/solution.py
@@ -24,15 +24,29 @@
     )
 
 
-def exchange(gate, up, rw, gain, fg, fu, sc_out, sr,
-             x, w, xn, ml, parts, sc, rr, s, r, own, rpiece, rparts, rrow, rall,
-             in_sem, a_send, a_recv, b_send, b_recv, s_send, s_recv, p_send, p_recv, o_send, o_recv):
+def exchange(gate, up, rw_in, gain_in, fg, fu, sg, su, sr,
+             rw, gain, x, w, xn, ml, parts, sc, rr, s, r, own, rpiece, rparts, rrow, rall,
+             r_sem, in_sem, a_send, a_recv, b_send, b_recv, s_send, s_recv, p_send, p_recv, o_send, o_recv):
     me = lax.axis_index("rows")
     us = lax.axis_index("owner")
     par = lax.rem(me, 2)
 
     def peer(k):
         return lax.rem(me + k, ROWS)
+
+    barrier = pltpu.get_barrier_semaphore()
+
+    def signal_rows(k, _):
+        pl.semaphore_signal(barrier, inc=1, device_id={"rows": peer(k)}, device_id_type=MESH)
+        return 0
+
+    lax.fori_loop(1, ROWS, signal_rows, 0)
+
+    def signal_owner(k, _):
+        pl.semaphore_signal(barrier, inc=1, device_id={"owner": lax.rem(us + k, OWNERS)}, device_id_type=MESH)
+        return 0
+
+    lax.fori_loop(1, OWNERS, signal_owner, 0)
 
     loads = []
     for e in range(E):
@@ -40,28 +54,20 @@
             cp = pltpu.make_async_copy(ref.at[e], x.at[a, e], in_sem.at[a, e])
             cp.start()
             loads.append((a, e, cp))
-    barrier = pltpu.get_barrier_semaphore()
-
-    def signal_rows(k, _):
-        pl.semaphore_signal(barrier, inc=1, device_id={"rows": peer(k)}, device_id_type=MESH)
-        return 0
-
-    lax.fori_loop(1, ROWS, signal_rows, 0)
-
-    def signal_owner(k, _):
-        pl.semaphore_signal(barrier, inc=1, device_id={"owner": lax.rem(us + k, OWNERS)}, device_id_type=MESH)
-        return 0
-
-    lax.fori_loop(1, OWNERS, signal_owner, 0)
-
-    part = rw[...] * gain[...]
-    lane64 = lax.broadcasted_iota(jnp.int32, (E, 128), 1) // 64
-    rpiece[...] = jnp.where(lane64 == par, jnp.concatenate([part, part], axis=1), 0.0)
+    small = [pltpu.make_async_copy(rw_in, rw, r_sem.at[0]), pltpu.make_async_copy(gain_in, gain, r_sem.at[1])]
+    for cp in small:
+        cp.start()
+
     for m in range(8):
         i = lax.broadcasted_iota(jnp.int32, (128, 1024), 0) + m * 128
         k = lax.broadcasted_iota(jnp.int32, (128, 1024), 1)
         hit = (lax.rem(i, 8) == k // 128) & (i // 8 == lax.rem(k, 128))
         w[pl.ds(m * 128, 128), :] = jnp.where(hit, 1.0, 0.0).astype(jnp.bfloat16)
+    for cp in small:
+        cp.wait()
+    part = rw[...] * gain[...]
+    lane64 = lax.broadcasted_iota(jnp.int32, (E, 128), 1) // 64
+    rpiece[...] = jnp.where(lane64 == par, jnp.concatenate([part, part], axis=1), 0.0)
     for a, e, cp in loads:
         cp.wait()
         m = jnp.max(jnp.abs(x[a, e]), axis=0, keepdims=True)
@@ -152,9 +158,9 @@
     first = (C * me) // 128
     second = jnp.minimum(first + 1, TILES - 1)
     shift = lax.rem(256 - (C * me - 128 * first), 256)
-    for a in range(2):
+    for a, ref in enumerate((sg, su)):
         both = jnp.concatenate([sc[a * TILES + first], sc[a * TILES + second]], axis=1)
-        sc_out[a] = pltpu.roll(both, shift, 1)[:, :128]
+        ref[...] = pltpu.roll(both, shift, 1)[:, :C]
 
     def wait_router(k, _):
         src = peer(k)
@@ -181,13 +187,13 @@
         fu[:, at] = pltpu.roll(jnp.where(lane, odd, even), 64, 1).astype(jnp.bfloat16)
         return 0
 
-    lax.fori_loop(1, ROWS // 2 + 1, merge, 0)
-
+    lax.fori_loop(1, 13, merge, 0)
     for k in range(1, OWNERS):
         src = lax.rem(us + k, OWNERS)
         remote(rrow, rall.at[src], o_send.at[k], o_recv.at[src], owner=src).wait_recv()
     for o in range(OWNERS):
         sr[o * E:(o + 1) * E, :] = rall[o].astype(jnp.bfloat16)
+    lax.fori_loop(13, ROWS // 2 + 1, merge, 0)
 
     def drain_a(q, _):
         @pl.when(owner_of(q) != me)
@@ -229,20 +235,23 @@
 
 def shards(master_gate, master_up, router_weight, router_gain):
     f32, bf16 = jnp.float32, jnp.bfloat16
-    vmem, any_ = pl.BlockSpec(memory_space=pltpu.VMEM), pl.BlockSpec(memory_space=pl.ANY)
+    vmem, any_, hbm = (pl.BlockSpec(memory_space=m) for m in (pltpu.VMEM, pl.ANY, pltpu.HBM))
     dma, scratch = pltpu.SemaphoreType.DMA, pltpu.VMEM
-    fg, fu, sc, sr = pl.pallas_call(
+    fg, fu, sg, su, sr = pl.pallas_call(
         exchange,
         name="exchange",
         out_shape=(
             jax.ShapeDtypeStruct((MSG, ROWS * R), bf16),
             jax.ShapeDtypeStruct((MSG, ROWS * R), bf16),
-            jax.ShapeDtypeStruct((2, E, 128), f32),
+            jax.ShapeDtypeStruct((E, C), f32),
+            jax.ShapeDtypeStruct((E, C), f32),
             jax.ShapeDtypeStruct((OWNERS * E, ROWS * R), bf16),
         ),
-        in_specs=[any_, any_, vmem, vmem],
-        out_specs=(vmem,) * 4,
+        in_specs=[hbm] * 4,
+        out_specs=(vmem,) * 5,
         scratch_shapes=[
+            scratch((E, R), f32),
+            scratch((1, R), f32),
             scratch((2, E, R, D), f32),
             scratch((1024, 1024), bf16),
             scratch((256, 1024), bf16),
@@ -257,23 +266,23 @@
             scratch((ROWS, E, 128), f32),
             scratch((E, ROWS * R), f32),
             scratch((OWNERS, E, ROWS * R), f32),
-            dma((2, E)), dma((Q,)), dma((ROWS,)), dma((ROWS,)), dma((Q,)),
+            dma((2,)), dma((2, E)), dma((Q,)), dma((ROWS,)), dma((ROWS,)), dma((Q,)),
             dma((ROWS,)), dma((ROWS,)), dma((ROWS,)), dma((ROWS,)), dma((OWNERS,)), dma((OWNERS,)),
         ],
         compiler_params=pltpu.CompilerParams(
             collective_id=0, has_side_effects=True, vmem_limit_bytes=40 * 2**20
         ),
-    )(master_gate, master_up, router_weight.T, router_gain[None, :])
-    sg, su = sc[0, :, :C], sc[1, :, :C]
+    )(*(pltpu.with_memory_space_constraint(v, pltpu.HBM) for v in (master_gate, master_up, router_weight.T, router_gain[None, :])))
     fg, fu = fg.reshape(C, E, ROWS * R), fu.reshape(C, E, ROWS * R)
     ins = (fg, fu, sg, su, sr)
     fg, fu, sg, su, sr = pl.pallas_call(
         put_out,
         name="put_out",
         out_shape=tuple(jax.ShapeDtypeStruct(i.shape, i.dtype) for i in ins),
-        in_specs=[vmem] * 5,
-        out_specs=(any_,) * 5,
+        in_specs=[any_] * 5,
+        out_specs=(hbm,) * 5,
         scratch_shapes=[dma((5,))],
+        compiler_params=pltpu.CompilerParams(vmem_limit_bytes=2**20),
     )(*ins)
     return fg.transpose(1, 2, 0), fu.transpose(1, 2, 0), sg, su, sr.T
 

time: 109 us -> 96.7 us (0.89); the launches traced: 108 us -> 95 us
  local copies, waits for them, and re-layouts: 8.49 us -> 0 us
  Pallas kernels: 99.3 us -> 94.4 us
    unnamed x14 -> x0, local copies, waits for them, and re-layouts: 7.89 us -> none
    pallas_call x1, Pallas kernels: 95.8 us -> 92.7 us  [shards(): pl.pallas_call(exchange, name='exchange', out_shape=(jax.ShapeDtypeStruct...]
    pallas_call x1, Pallas kernels: 3.53 us -> 1.71 us  [shards(): pl.pallas_call(put_out, name='put_out', out_shape=tuple((jax.ShapeDtypeSt...]
where the time goes in v2:
time: 96.7 us; the launch traced here: 95 us
  Pallas kernels  94.4 us (98%)
    pallas_call x1, Pallas kernels, shards(): pl.pallas_call(exchange, name='exchange', out_shape=(jax.ShapeDtypeStruct...  92.7 us

profile of v2, /device:TPU:14, one launch (start us, length us, event | category | flops | bytes accessed | tf_op | source)
XLA Modules:
  0.0 95.0 jit_solution(9703694577719762378)
XLA Ops:
  0.6 92.7 %exchange.1 = (bf16[352,2048]{1,0:T(8,128)(2,1)S(1)}, bf16[352,2048]{1,0:T(8,128)(2,1)S(1)}, f32[8,44]{1,0:T(8,128)S(1)}, f32[8,44]{1,0:T(8,128)S(1)}, bf16[64,2048]{1,0:T(8,128)(2,1)S(1)}) custom-call(f32[8,64,1408]{2,1,0:T(8,128)} %gate.1, f32[8,64,1408]{2,1,0:T(8,128)} %up.1, f32[8,64]{1,0:T(8,128)} %bitcast.9, f32[1,64]{1,0:T(1,128)} %bitcast.10), custom_call_target="tpu_custom_call" | custom-call | tf_op jit(solution)/shard_map/exchange/pallas_call | solution.py:240
  93.3 1.7 %put_out.1 = (bf16[44,8,2048]{2,1,0:T(8,128)(2,1)}, bf16[44,8,2048]{2,1,0:T(8,128)(2,1)}, f32[8,44]{1,0:T(8,128)}, f32[8,44]{1,0:T(8,128)}, bf16[64,2048]{1,0:T(8,128)(2,1)}) custom-call(bf16[44,8,2048]{2,1,0:T(8,128)(2,1)S(1)} %bitcast.7, bf16[44,8,2048]{2,1,0:T(8,128)(2,1)S(1)} %bitcast.8, f32[8,44]{1,0:T(8,128)S(1)} %get-tuple-element.17.refs_2_, ...), custom_call_target="tpu_custom_call" | custom-call | tf_op jit(solution)/shard_map/put_out/pallas_call | solution.py:278

commit v3 on v2

--- a/solution.py
+++ b/solution.py
@@ -15,7 +15,7 @@
 
 
 def owner_of(q):
-    return (q * 16) // 11
+    return (ROWS * lax.rem(q, TILES)) // TILES + q // TILES
 
 
 def remote(src, dst, send, recv, **where):
@@ -58,11 +58,6 @@
     for cp in small:
         cp.start()
 
-    for m in range(8):
-        i = lax.broadcasted_iota(jnp.int32, (128, 1024), 0) + m * 128
-        k = lax.broadcasted_iota(jnp.int32, (128, 1024), 1)
-        hit = (lax.rem(i, 8) == k // 128) & (i // 8 == lax.rem(k, 128))
-        w[pl.ds(m * 128, 128), :] = jnp.where(hit, 1.0, 0.0).astype(jnp.bfloat16)
     for cp in small:
         cp.wait()
     part = rw[...] * gain[...]
@@ -99,8 +94,16 @@
     lax.fori_loop(1, ROWS, send_router, 0)
     rparts[pl.ds(me, 1)] = rpiece[...][None]
 
-    mine = (11 * me + 15) // 16
-    is_owner = owner_of(mine) == me
+    for m in range(8):
+        i = lax.broadcasted_iota(jnp.int32, (128, 1024), 0) + m * 128
+        k = lax.broadcasted_iota(jnp.int32, (128, 1024), 1)
+        hit = (lax.rem(i, 8) == k // 128) & (i // 8 == lax.rem(k, 128))
+        w[pl.ds(m * 128, 128), :] = jnp.where(hit, 1.0, 0.0).astype(jnp.bfloat16)
+    gate_tile, up_tile = (TILES * me + ROWS - 1) // ROWS, (TILES * (me - 1) + ROWS - 1) // ROWS
+    owns_gate = (ROWS * gate_tile) // TILES == me
+    owns_up = (me > 0) & ((ROWS * up_tile) // TILES == me - 1)
+    is_owner = (owns_gate & (gate_tile < TILES)) | owns_up
+    mine = jnp.where(owns_up, TILES + up_tile, gate_tile)
 
     @pl.when(is_owner)
     def _():
@@ -125,33 +128,51 @@
 
         return 0
 
-    lax.fori_loop(0, Q, wait_scale, 0)
-    rr[...] = 1.0 / sc[...]
-
-    for t0 in range(0, TILES, 2):
-        n = min(2, TILES - t0)
-        for i in range(n):
-            t = t0 + i
+    def tile_scales(t):
+        for q in (t, TILES + t):
+            wait_scale(q, 0)
+            rr[pl.ds(q, 1)] = 1.0 / sc[pl.ds(q, 1)]
+
+    def block(j):
+        return s.at[pl.ds(pl.multiple_of(j * MSG, 32), MSG)]
+
+    def send_block(k, _):
+        to = peer(k)
+        remote(block(to), r.at[me], s_send.at[k], s_recv.at[me], rows=to).start()
+        return 0
+
+    def send_block_down(k, _):
+        return send_block(ROWS - k, _)
+
+    right, left = C * (me + 1), C * (me + ROWS)
+    right_tile, left_tile = right // 128, (left - 1) // 128
+    right_sent, left_sent = 0, 0
+    for step in range(6):
+        tiles = (lax.rem(right_tile + step, TILES), lax.rem(left_tile - step, TILES))
+        tile_scales(tiles[0])
+        pl.when(tiles[0] != tiles[1])(lambda t=tiles[1]: tile_scales(t))
+        for i, t in enumerate(tiles):
+            lanes = pl.ds(pl.multiple_of(t * 128, 128), 128)
             for h in range(2):
                 a = lax.rem(par + h, 2)
                 for e in range(E):
-                    v = x[a, e, :, t * 128:(t + 1) * 128] * rr[a * TILES + t, pl.ds(e, 1), :]
-                    xn[pl.ds(i * 128 + h * 64, 64), e * 128:(e + 1) * 128] = v.astype(jnp.bfloat16)
+                    v = x[a, e, :, lanes] * rr[a * TILES + t, pl.ds(e, 1), :]
+                    xn[i * 128 + h * 64:i * 128 + (h + 1) * 64, e * 128:(e + 1) * 128] = v.astype(jnp.bfloat16)
         out = lax.dot_general(
-            w[...], xn[:n * 128, :], (((1,), (1,)), ((), ())), preferred_element_type=jnp.float32
+            w[...], xn[...], (((1,), (1,)), ((), ())), preferred_element_type=jnp.float32
         )
-        for i in range(n):
-            s[pl.ds((t0 + i) * 1024, 1024), :] = out[:, i * 128:(i + 1) * 128].astype(jnp.bfloat16)
-
-    def block(j):
-        return s.at[pl.ds(pl.multiple_of(j * MSG, 32), MSG)]
-
-    def send_block(k, _):
-        to = peer(k)
-        remote(block(to), r.at[me], s_send.at[k], s_recv.at[me], rows=to).start()
-        return 0
-
-    lax.fori_loop(1, ROWS, send_block, 0)
+        for i, t in enumerate(tiles):
+            at = pl.ds(pl.multiple_of(t * 1024, 1024), 1024)
+            s[at, :] = out[:, i * 128:(i + 1) * 128].astype(jnp.bfloat16)
+        if step < 5:
+            right_done = (128 * (right_tile + step + 1) - right) // C
+            left_done = (left - 128 * (left_tile - step)) // C
+        else:
+            right_done, left_done = ROWS // 2, ROWS // 2 - 1
+        lax.fori_loop(right_sent + 1, right_done + 1, send_block, 0)
+        lax.fori_loop(left_sent + 1, left_done + 1, send_block_down, 0)
+        right_sent, left_sent = right_done, left_done
+
     keep = pltpu.make_async_copy(block(me), r.at[me], s_recv.at[me])
     keep.start()
 
@@ -178,7 +199,7 @@
     lane = lax.broadcasted_iota(jnp.int32, (MSG, 128), 1) < 64
 
     def merge(kk, _):
-        p = lax.rem(me // 2 - kk + 16, 16)
+        p = lax.rem(me // 2 + 16 + lax.rem(kk, 2) * ((kk + 1) // 2) - (1 - lax.rem(kk, 2)) * (kk // 2), 16)
         for src in (2 * p, 2 * p + 1):
             pltpu.make_async_copy(r.at[src], r.at[src], s_recv.at[src]).wait()
         even, odd = r[2 * p].astype(jnp.float32), r[2 * p + 1].astype(jnp.float32)
@@ -187,13 +208,13 @@
         fu[:, at] = pltpu.roll(jnp.where(lane, odd, even), 64, 1).astype(jnp.bfloat16)
         return 0
 
-    lax.fori_loop(1, 13, merge, 0)
+    lax.fori_loop(0, 12, merge, 0)
     for k in range(1, OWNERS):
         src = lax.rem(us + k, OWNERS)
         remote(rrow, rall.at[src], o_send.at[k], o_recv.at[src], owner=src).wait_recv()
     for o in range(OWNERS):
         sr[o * E:(o + 1) * E, :] = rall[o].astype(jnp.bfloat16)
-    lax.fori_loop(13, ROWS // 2 + 1, merge, 0)
+    lax.fori_loop(12, ROWS // 2, merge, 0)
 
     def drain_a(q, _):
         @pl.when(owner_of(q) != me)

time: 96.7 us -> 94.4 us (0.976); the launches traced: 95 us -> 94.2 us
  no operation moved by 1% of the time
where the time goes in v3:
time: 94.4 us; the launch traced here: 94.2 us
  Pallas kernels  93.6 us (99%)
    pallas_call x1, Pallas kernels, shards(): pl.pallas_call(exchange, name='exchange', out_shape=(jax.ShapeDtypeStruct...  91.9 us

profile of v3, /device:TPU:14, one launch (start us, length us, event | category | flops | bytes accessed | tf_op | source)
XLA Modules:
  0.0 94.2 jit_solution(7020001362340111400)
XLA Ops:
  0.6 91.9 %exchange.1 = (bf16[352,2048]{1,0:T(8,128)(2,1)S(1)}, bf16[352,2048]{1,0:T(8,128)(2,1)S(1)}, f32[8,44]{1,0:T(8,128)S(1)}, f32[8,44]{1,0:T(8,128)S(1)}, bf16[64,2048]{1,0:T(8,128)(2,1)S(1)}) custom-call(f32[8,64,1408]{2,1,0:T(8,128)} %gate.1, f32[8,64,1408]{2,1,0:T(8,128)} %up.1, f32[8,64]{1,0:T(8,128)} %bitcast.9, f32[1,64]{1,0:T(1,128)} %bitcast.10), custom_call_target="tpu_custom_call" | custom-call | tf_op jit(solution)/shard_map/exchange/pallas_call | solution.py:261
  92.5 1.7 %put_out.1 = (bf16[44,8,2048]{2,1,0:T(8,128)(2,1)}, bf16[44,8,2048]{2,1,0:T(8,128)(2,1)}, f32[8,44]{1,0:T(8,128)}, f32[8,44]{1,0:T(8,128)}, bf16[64,2048]{1,0:T(8,128)(2,1)}) custom-call(bf16[44,8,2048]{2,1,0:T(8,128)(2,1)S(1)} %bitcast.7, bf16[44,8,2048]{2,1,0:T(8,128)(2,1)S(1)} %bitcast.8, f32[8,44]{1,0:T(8,128)S(1)} %get-tuple-element.17.refs_2_, ...), custom_call_target="tpu_custom_call" | custom-call | tf_op jit(solution)/shard_map/put_out/pallas_call | solution.py:299

commit v4 on v3

--- a/solution.py
+++ b/solution.py
@@ -12,6 +12,7 @@
 TILES = D // 128
 Q = 2 * TILES
 MSG = C * E
+START = 2
 
 
 def owner_of(q):
@@ -34,19 +35,8 @@
     def peer(k):
         return lax.rem(me + k, ROWS)
 
-    barrier = pltpu.get_barrier_semaphore()
-
-    def signal_rows(k, _):
-        pl.semaphore_signal(barrier, inc=1, device_id={"rows": peer(k)}, device_id_type=MESH)
-        return 0
-
-    lax.fori_loop(1, ROWS, signal_rows, 0)
-
-    def signal_owner(k, _):
-        pl.semaphore_signal(barrier, inc=1, device_id={"owner": lax.rem(us + k, OWNERS)}, device_id_type=MESH)
-        return 0
-
-    lax.fori_loop(1, OWNERS, signal_owner, 0)
+    def far(k):
+        return ROWS // 2 + lax.rem(k, 2) * (k // 2) - (1 - lax.rem(k, 2)) * (k // 2)
 
     loads = []
     for e in range(E):
@@ -54,6 +44,20 @@
             cp = pltpu.make_async_copy(ref.at[e], x.at[a, e], in_sem.at[a, e])
             cp.start()
             loads.append((a, e, cp))
+    barrier = pltpu.get_barrier_semaphore()
+
+    def signal_rows(k, _):
+        pl.semaphore_signal(barrier, inc=1, device_id={"rows": peer(far(k))}, device_id_type=MESH)
+        return 0
+
+    lax.fori_loop(1, ROWS, signal_rows, 0)
+
+    def signal_owner(k, _):
+        pl.semaphore_signal(barrier, inc=1, device_id={"owner": lax.rem(us + k, OWNERS)}, device_id_type=MESH)
+        return 0
+
+    lax.fori_loop(1, OWNERS, signal_owner, 0)
+
     small = [pltpu.make_async_copy(rw_in, rw, r_sem.at[0]), pltpu.make_async_copy(gain_in, gain, r_sem.at[1])]
     for cp in small:
         cp.start()
@@ -71,20 +75,26 @@
 
     pl.semaphore_wait(barrier, ROWS - 1 + OWNERS - 1)
 
-    def send_part(q, _):
-        to = owner_of(q)
-
-        @pl.when(to != me)
+    def owned(d):
+        gate_tile, up_tile = (TILES * d + ROWS - 1) // ROWS, (TILES * (d - 1) + ROWS - 1) // ROWS
+        owns_up = (d > 0) & ((ROWS * up_tile) // TILES == d - 1)
+        owns_gate = (gate_tile < TILES) & ((ROWS * gate_tile) // TILES == d)
+        return owns_gate | owns_up, jnp.where(owns_up, TILES + up_tile, jnp.minimum(gate_tile, TILES - 1))
+
+    is_owner, mine = owned(me)
+
+    def send_part(k, _):
+        to = peer(far(k))
+        wanted, q = owned(to)
+
+        @pl.when(wanted)
         def _():
             remote(ml.at[q], parts.at[me], a_send.at[q], a_recv.at[me], rows=to).start()
 
-        @pl.when(to == me)
-        def _():
-            parts[pl.ds(me, 1)] = ml[pl.ds(q, 1)]
-
-        return 0
-
-    lax.fori_loop(0, Q, send_part, 0)
+        return 0
+
+    lax.fori_loop(1, ROWS, send_part, 0)
+    parts[pl.ds(me, 1)] = ml[pl.ds(mine, 1)]
 
     def send_router(k, _):
         to = peer(k)
@@ -99,12 +109,6 @@
         k = lax.broadcasted_iota(jnp.int32, (128, 1024), 1)
         hit = (lax.rem(i, 8) == k // 128) & (i // 8 == lax.rem(k, 128))
         w[pl.ds(m * 128, 128), :] = jnp.where(hit, 1.0, 0.0).astype(jnp.bfloat16)
-    gate_tile, up_tile = (TILES * me + ROWS - 1) // ROWS, (TILES * (me - 1) + ROWS - 1) // ROWS
-    owns_gate = (ROWS * gate_tile) // TILES == me
-    owns_up = (me > 0) & ((ROWS * up_tile) // TILES == me - 1)
-    is_owner = (owns_gate & (gate_tile < TILES)) | owns_up
-    mine = jnp.where(owns_up, TILES + up_tile, gate_tile)
-
     @pl.when(is_owner)
     def _():
         def wait_part(k, _):
@@ -116,7 +120,7 @@
         sc[pl.ds(mine, 1)] = jnp.max(parts[...], axis=0, keepdims=True)
 
         def send_scale(k, _):
-            remote(sc.at[mine], sc.at[mine], b_send.at[k], b_recv.at[mine], rows=peer(k)).start()
+            remote(sc.at[mine], sc.at[mine], b_send.at[k], b_recv.at[mine], rows=peer(far(k))).start()
             return 0
 
         lax.fori_loop(1, ROWS, send_scale, 0)
@@ -146,8 +150,17 @@
 
     right, left = C * (me + 1), C * (me + ROWS)
     right_tile, left_tile = right // 128, (left - 1) // 128
-    right_sent, left_sent = 0, 0
-    for step in range(6):
+
+    def first(step):
+        if step == 0:
+            return 0, 0
+        return (
+            (128 * (right_tile + step) - right + C - 1) // C,
+            (left - 128 * (left_tile - step + 1) + C - 1) // C,
+        )
+
+    right_sent, left_sent = first(START)
+    for step in (*range(START, 6), *range(START - 1, -1, -1)):
         tiles = (lax.rem(right_tile + step, TILES), lax.rem(left_tile - step, TILES))
         tile_scales(tiles[0])
         pl.when(tiles[0] != tiles[1])(lambda t=tiles[1]: tile_scales(t))
@@ -164,11 +177,13 @@
         for i, t in enumerate(tiles):
             at = pl.ds(pl.multiple_of(t * 1024, 1024), 1024)
             s[at, :] = out[:, i * 128:(i + 1) * 128].astype(jnp.bfloat16)
-        if step < 5:
+        if step < START:
+            (right_sent, left_sent), (right_done, left_done) = first(step), first(step + 1)
+        elif step == 5:
+            right_done, left_done = ROWS // 2, ROWS // 2 - 1
+        else:
             right_done = (128 * (right_tile + step + 1) - right) // C
             left_done = (left - 128 * (left_tile - step)) // C
-        else:
-            right_done, left_done = ROWS // 2, ROWS // 2 - 1
         lax.fori_loop(right_sent + 1, right_done + 1, send_block, 0)
         lax.fori_loop(left_sent + 1, left_done + 1, send_block_down, 0)
         right_sent, left_sent = right_done, left_done
@@ -228,7 +243,7 @@
     @pl.when(is_owner)
     def _():
         def drain_b(k, _):
-            remote(sc.at[mine], sc.at[mine], b_send.at[k], b_recv.at[mine], rows=peer(k)).wait_send()
+            remote(sc.at[mine], sc.at[mine], b_send.at[k], b_recv.at[mine], rows=peer(far(k))).wait_send()
             return 0
 
         lax.fori_loop(1, ROWS, drain_b, 0)
@@ -247,7 +262,10 @@
 
 def put_out(*refs):
     ins, outs, sem = refs[:5], refs[5:10], refs[10]
-    copies = [pltpu.make_async_copy(i, o, sem.at[n]) for n, (i, o) in enumerate(zip(ins, outs))]
+    pieces = [(i, o) for i, o in zip(ins[2:], outs[2:])]
+    for i, o in zip(ins[:2], outs[:2]):
+        pieces += [(i.at[pl.ds(c, C // 4)], o.at[pl.ds(c, C // 4)]) for c in range(0, C, C // 4)]
+    copies = [pltpu.make_async_copy(i, o, sem.at[n]) for n, (i, o) in enumerate(pieces)]
     for cp in copies:
         cp.start()
     for cp in copies:
@@ -302,7 +320,7 @@
         out_shape=tuple(jax.ShapeDtypeStruct(i.shape, i.dtype) for i in ins),
         in_specs=[any_] * 5,
         out_specs=(hbm,) * 5,
-        scratch_shapes=[dma((5,))],
+        scratch_shapes=[dma((11,))],
         compiler_params=pltpu.CompilerParams(vmem_limit_bytes=2**20),
     )(*ins)
     return fg.transpose(1, 2, 0), fu.transpose(1, 2, 0), sg, su, sr.T

time: 94.4 us -> 94 us (level)
  Pallas kernels: 93.6 us -> 92.5 us
    pallas_call x1, Pallas kernels: 91.9 us -> 90.7 us  [shards(): pl.pallas_call(exchange, name='exchange', out_shape=(jax.ShapeDtypeStruct...]
where the time goes in v4:
time: 94 us; the launch traced here: 93.1 us
  Pallas kernels  92.5 us (98%)
    pallas_call x1, Pallas kernels, shards(): pl.pallas_call(exchange, name='exchange', out_shape=(jax.ShapeDtypeStruct...  90.7 us

profile of v4, /device:TPU:14, one launch (start us, length us, event | category | flops | bytes accessed | tf_op | source)
XLA Modules:
  0.0 93.1 jit_solution(16533252219902124895)
XLA Ops:
  0.6 90.7 %exchange.1 = (bf16[352,2048]{1,0:T(8,128)(2,1)S(1)}, bf16[352,2048]{1,0:T(8,128)(2,1)S(1)}, f32[8,44]{1,0:T(8,128)S(1)}, f32[8,44]{1,0:T(8,128)S(1)}, bf16[64,2048]{1,0:T(8,128)(2,1)S(1)}) custom-call(f32[8,64,1408]{2,1,0:T(8,128)} %gate.1, f32[8,64,1408]{2,1,0:T(8,128)} %up.1, f32[8,64]{1,0:T(8,128)} %bitcast.9, f32[1,64]{1,0:T(1,128)} %bitcast.10), custom_call_target="tpu_custom_call" | custom-call | tf_op jit(solution)/shard_map/exchange/pallas_call | solution.py:279
  91.3 1.8 %put_out.1 = (bf16[44,8,2048]{2,1,0:T(8,128)(2,1)}, bf16[44,8,2048]{2,1,0:T(8,128)(2,1)}, f32[8,44]{1,0:T(8,128)}, f32[8,44]{1,0:T(8,128)}, bf16[64,2048]{1,0:T(8,128)(2,1)}) custom-call(bf16[44,8,2048]{2,1,0:T(8,128)(2,1)S(1)} %bitcast.7, bf16[44,8,2048]{2,1,0:T(8,128)(2,1)S(1)} %bitcast.8, f32[8,44]{1,0:T(8,128)S(1)} %get-tuple-element.17.refs_2_, ...), custom_call_target="tpu_custom_call" | custom-call | tf_op jit(solution)/shard_map/put_out/pallas_call | solution.py:317

commit v5 on v4

--- a/solution.py
+++ b/solution.py
@@ -211,9 +211,33 @@
         remote(rrow, rall.at[us], o_send.at[k], o_recv.at[us], owner=to).start()
     rall[pl.ds(us, 1)] = rrow[...][None]
 
+    def drain_a(q, _):
+        @pl.when(owner_of(q) != me)
+        def _():
+            remote(ml.at[q], parts.at[me], a_send.at[q], a_recv.at[me], rows=owner_of(q)).wait_send()
+
+        return 0
+
+    lax.fori_loop(0, Q, drain_a, 0)
+
+    @pl.when(is_owner)
+    def _():
+        def drain_b(k, _):
+            remote(sc.at[mine], sc.at[mine], b_send.at[k], b_recv.at[mine], rows=peer(far(k))).wait_send()
+            return 0
+
+        lax.fori_loop(1, ROWS, drain_b, 0)
+
+    def drain_router(k, _):
+        remote(rpiece, rparts.at[me], p_send.at[k], p_recv.at[me], rows=peer(k)).wait_send()
+        return 0
+
+    lax.fori_loop(1, ROWS, drain_router, 0)
+
     lane = lax.broadcasted_iota(jnp.int32, (MSG, 128), 1) < 64
 
-    def merge(kk, _):
+    def merge(n, _):
+        kk = jnp.where(n < 11, n + 5, 15 - n)
         p = lax.rem(me // 2 + 16 + lax.rem(kk, 2) * ((kk + 1) // 2) - (1 - lax.rem(kk, 2)) * (kk // 2), 16)
         for src in (2 * p, 2 * p + 1):
             pltpu.make_async_copy(r.at[src], r.at[src], s_recv.at[src]).wait()
@@ -229,35 +253,17 @@
         remote(rrow, rall.at[src], o_send.at[k], o_recv.at[src], owner=src).wait_recv()
     for o in range(OWNERS):
         sr[o * E:(o + 1) * E, :] = rall[o].astype(jnp.bfloat16)
-    lax.fori_loop(12, ROWS // 2, merge, 0)
-
-    def drain_a(q, _):
-        @pl.when(owner_of(q) != me)
-        def _():
-            remote(ml.at[q], parts.at[me], a_send.at[q], a_recv.at[me], rows=owner_of(q)).wait_send()
-
-        return 0
-
-    lax.fori_loop(0, Q, drain_a, 0)
-
-    @pl.when(is_owner)
-    def _():
-        def drain_b(k, _):
-            remote(sc.at[mine], sc.at[mine], b_send.at[k], b_recv.at[mine], rows=peer(far(k))).wait_send()
-            return 0
-
-        lax.fori_loop(1, ROWS, drain_b, 0)
-
-    def drain(k, _):
-        to = peer(k)
-        remote(rpiece, rparts.at[me], p_send.at[k], p_recv.at[me], rows=to).wait_send()
-        remote(block(to), r.at[me], s_send.at[k], s_recv.at[me], rows=to).wait_send()
-        return 0
-
-    lax.fori_loop(1, ROWS, drain, 0)
     for k in range(1, OWNERS):
         to = lax.rem(us + k, OWNERS)
         remote(rrow, rall.at[us], o_send.at[k], o_recv.at[us], owner=to).wait_send()
+    lax.fori_loop(12, ROWS // 2, merge, 0)
+
+    def drain(k, _):
+        to = peer(k)
+        remote(block(to), r.at[me], s_send.at[k], s_recv.at[me], rows=to).wait_send()
+        return 0
+
+    lax.fori_loop(1, ROWS, drain, 0)
 
 
 def put_out(*refs):

time: 94 us -> 92.3 us (0.982)
  Pallas kernels: 92.5 us -> 91.4 us
    pallas_call x1, Pallas kernels: 90.7 us -> 89.7 us  [shards(): pl.pallas_call(exchange, name='exchange', out_shape=(jax.ShapeDtypeStruct...]
where the time goes in v5:
time: 92.3 us; the launch traced here: 92.1 us
  Pallas kernels  91.4 us (99%)
    pallas_call x1, Pallas kernels, shards(): pl.pallas_call(exchange, name='exchange', out_shape=(jax.ShapeDtypeStruct...  89.7 us

profile of v5, /device:TPU:14, one launch (start us, length us, event | category | flops | bytes accessed | tf_op | source)
XLA Modules:
  0.0 92.1 jit_solution(18414273269807455792)
XLA Ops:
  0.6 89.7 %exchange.1 = (bf16[352,2048]{1,0:T(8,128)(2,1)S(1)}, bf16[352,2048]{1,0:T(8,128)(2,1)S(1)}, f32[8,44]{1,0:T(8,128)S(1)}, f32[8,44]{1,0:T(8,128)S(1)}, bf16[64,2048]{1,0:T(8,128)(2,1)S(1)}) custom-call(f32[8,64,1408]{2,1,0:T(8,128)} %gate.1, f32[8,64,1408]{2,1,0:T(8,128)} %up.1, f32[8,64]{1,0:T(8,128)} %bitcast.9, f32[1,64]{1,0:T(1,128)} %bitcast.10), custom_call_target="tpu_custom_call" | custom-call | tf_op jit(solution)/shard_map/exchange/pallas_call | solution.py:285
  90.3 1.8 %put_out.1 = (bf16[44,8,2048]{2,1,0:T(8,128)(2,1)}, bf16[44,8,2048]{2,1,0:T(8,128)(2,1)}, f32[8,44]{1,0:T(8,128)}, f32[8,44]{1,0:T(8,128)}, bf16[64,2048]{1,0:T(8,128)(2,1)}) custom-call(bf16[44,8,2048]{2,1,0:T(8,128)(2,1)S(1)} %bitcast.7, bf16[44,8,2048]{2,1,0:T(8,128)(2,1)S(1)} %bitcast.8, f32[8,44]{1,0:T(8,128)S(1)} %get-tuple-element.17.refs_2_, ...), custom_call_target="tpu_custom_call" | custom-call | tf_op jit(solution)/shard_map/put_out/pallas_call | solution.py:323
